TPU v7x, 32 devices: a whole 2x2x4 slice. The times are simulated.
32 devices in a mesh: dp: 2 (over x), ctx: 4 (over y, core), tp: 4 (over z).
Axes of the slice: x: 2, y: 2, z: 4, core: 2. Of those that a mesh axis runs over, the one named last changes fastest.
Arguments:
- block_input: bfloat16 [2, 8, 256, 2048], P('dp', 'ctx', 'tp'), may hold values from -6 to 6
- block_order: int32 [2, 8], P('dp'), may hold values from 0 to 7, each once within a row
- w_qkv: bfloat16 [2048, 3, 2048], P(('dp', 'ctx'), None, 'tp'), may hold values from -1 to 1
- w_out: bfloat16 [2048, 2048], P('tp', ('dp', 'ctx')), may hold values from -3 to 3
- gain_attn: bfloat16 [2048], P(('dp', 'ctx')), may hold values from 0.5 to 1.5
- w_gate_up: bfloat16 [2048, 2, 8192], P(('dp', 'ctx'), None, 'tp'), may hold values from -0.125 to 0.125
- w_down: bfloat16 [8192, 2048], P('tp', ('dp', 'ctx')), may hold values from -0.0625 to 0.0625
- gain_mlp: bfloat16 [2048], P(('dp', 'ctx')), may hold values from 0.5 to 1.5
- cotangent: bfloat16 [2, 8, 256, 2048], P('dp', 'ctx', 'tp'), may hold values from -6 to 6
Outputs:
- block_output: bfloat16 [2, 8, 256, 2048], P('dp', 'ctx', 'tp')
- input_grad: float32 [2, 8, 256, 2048], P('dp', 'ctx', 'tp')
- grad_qkv: float32 [2048, 3, 2048], P(('dp', 'ctx'), None, 'tp')
- grad_out: float32 [2048, 2048], P('tp', ('dp', 'ctx'))
- grad_gain_attn: float32 [2048], P(('dp', 'ctx'))
- grad_gate_up: float32 [2048, 2, 8192], P(('dp', 'ctx'), None, 'tp')
- grad_down: float32 [8192, 2048], P('tp', ('dp', 'ctx'))
- grad_gain_mlp: float32 [2048], P(('dp', 'ctx'))
Inputs may be any that keep to these rules, and one draw needn't show every extreme that they name: `block_order`: each row lists every block number of one sequence once.
All inputs are finite; a program needn't handle non-finite values.
Results may differ from a plain program's by a relative error of at most 0.019.
Values may be sent and summed in bfloat16 or wider, within the bound.
A program may use at most 192 MiB of HBM per device.

v0:
```python
import jax
import jax.numpy as jnp
from jax import lax
from jax.sharding import PartitionSpec as P

HEAD_DIM = 64
EPSILON = 1e-05
ROPE_BASE = 130000.0
NEG_LARGE = -1e30


def rope_tables(positions, head_size):
    half = head_size // 2
    freq = ROPE_BASE ** (-(jnp.arange(half, dtype=jnp.float32) * 2.0 / head_size))
    angle = positions.astype(jnp.float32)[..., None] * freq
    cosine = jnp.cos(angle)
    sine = jnp.sin(angle)
    return (jnp.concatenate([cosine, cosine], -1), jnp.concatenate([sine, sine], -1))


def rotate(values):
    half = values.shape[-1] // 2
    return jnp.concatenate([-values[..., half:], values[..., :half]], -1)


def unrotate(values):
    half = values.shape[-1] // 2
    return jnp.concatenate([values[..., half:], -values[..., :half]], -1)


def rope_apply(values, cosine, sine):
    return values * cosine + rotate(values) * sine


def rope_back(grads, cosine, sine):
    return grads * cosine + unrotate(grads * sine)


def gather_rows(values):
    return lax.all_gather(values, "tp", axis=2, tiled=True)


def sum_rows(values):
    return lax.psum_scatter(values, "tp", scatter_dimension=2, tiled=True)


def gather_cotangent(values):
    return lax.all_gather(values, "tp", axis=2, tiled=True)


def sum_normed(values):
    return lax.psum_scatter(values, "tp", scatter_dimension=2, tiled=True)


def block_scores(query, key_blk, query_pos, key_pos, head_count):
    key_heads = key_blk.reshape(key_blk.shape[0], head_count, HEAD_DIM)
    scores = jnp.einsum("qhe,khe->hqk", query, key_heads, preferred_element_type=jnp.float32)
    visible = key_pos[None, :] <= query_pos[:, None]
    return jnp.where(visible[None], scores, -jnp.inf)


def online_update(state, query, query_pos, key_blk, value_blk, key_pos, head_count):
    run_max, run_sum, run_acc = state
    scores = block_scores(query, key_blk, query_pos, key_pos, head_count)
    new_max = jnp.maximum(run_max, jnp.max(scores, -1))
    factor = jnp.exp(run_max - new_max)
    probs = jnp.exp(scores - new_max[..., None])
    new_sum = run_sum * factor + jnp.sum(probs, -1)
    value_heads = value_blk.reshape(value_blk.shape[0], head_count, HEAD_DIM).astype(jnp.float32)
    mixed = jnp.einsum("hqk,khe->qhe", probs, value_heads, precision=lax.Precision.HIGHEST)
    new_acc = run_acc * factor.T[:, :, None] + mixed
    return (new_max, new_sum, new_acc)


def backward_block(
    query, query_pos, grad_blk, log_total, delta, key_blk, value_blk, key_pos, head_count
):
    scores = block_scores(query, key_blk, query_pos, key_pos, head_count)
    probs = jnp.exp(scores - log_total[..., None])
    value_heads = value_blk.reshape(value_blk.shape[0], head_count, HEAD_DIM)
    key_heads = key_blk.reshape(key_blk.shape[0], head_count, HEAD_DIM)
    dprobs = jnp.einsum("qhe,khe->hqk", grad_blk, value_heads, preferred_element_type=jnp.float32)
    grad_scores = (probs * (dprobs - delta[..., None])).astype(jnp.bfloat16)
    grad_query = jnp.einsum(
        "hqk,khe->qhe", grad_scores, key_heads, preferred_element_type=jnp.float32
    )
    grad_key = jnp.einsum("hqk,qhe->khe", grad_scores, query, preferred_element_type=jnp.float32)
    grad_value = jnp.einsum(
        "hqk,qhe->khe", probs.astype(jnp.bfloat16), grad_blk, preferred_element_type=jnp.float32
    )
    flat_width = head_count * HEAD_DIM
    return (grad_query, grad_key.reshape(-1, flat_width), grad_value.reshape(-1, flat_width))


def body(block_input, block_order, w_qkv, w_out, gain_attn, w_gate_up, w_down, gain_mlp, cotangent):
    f32 = jnp.float32
    bf16 = jnp.bfloat16
    seq_count = block_input.shape[0]
    row_count = block_input.shape[2]
    span = row_count * lax.axis_size("tp")
    local_width = w_qkv.shape[2]
    head_count = local_width // HEAD_DIM
    query_rows = 2 * span
    block_total = block_order.shape[1]
    ctx_index = lax.axis_index("ctx")
    my_ids = lax.dynamic_slice_in_dim(block_order, ctx_index * 2, 2, 1)
    offsets = jnp.arange(span, dtype=jnp.int32)
    query_pos = (my_ids[:, :, None] * span + offsets).reshape(seq_count, query_rows)
    cosine, sine = rope_tables(query_pos, HEAD_DIM)
    cosine = cosine[:, :, None, :]
    sine = sine[:, :, None, :]
    full_qkv, full_out, full_gain_attn = (
        lax.all_gather(w_qkv, ("dp", "ctx"), axis=0, tiled=True),
        lax.all_gather(w_out, ("dp", "ctx"), axis=1, tiled=True),
        lax.all_gather(gain_attn, ("dp", "ctx"), axis=0, tiled=True),
    )
    x_float = block_input.astype(f32)
    rms_attn = lax.rsqrt(jnp.mean(x_float * x_float, -1, keepdims=True) + EPSILON)
    unit_attn = x_float * rms_attn
    normed_attn = (unit_attn * full_gain_attn.astype(f32)).astype(bf16)
    normed_attn_full = gather_rows(normed_attn)
    qkv = jnp.einsum("spcd,dte->spcte", normed_attn_full, full_qkv, preferred_element_type=f32)
    qkv = qkv.reshape(seq_count, query_rows, 3, head_count, HEAD_DIM)
    queries = (rope_apply(qkv[:, :, 0], cosine, sine) * 0.125).astype(bf16)
    keys = rope_apply(qkv[:, :, 1], cosine, sine).astype(bf16)
    values = qkv[:, :, 2].astype(bf16)
    key_send = keys.reshape(seq_count, 2, span, local_width)
    value_send = values.reshape(seq_count, 2, span, local_width)
    initial = (
        jnp.full((seq_count, head_count, query_rows), NEG_LARGE, f32),
        jnp.zeros((seq_count, head_count, query_rows), f32),
        jnp.zeros((seq_count, query_rows, head_count, HEAD_DIM), f32),
    )
    key_piece = lax.all_gather(key_send, "ctx", axis=1, tiled=True)
    value_piece = lax.all_gather(value_send, "ctx", axis=1, tiled=True)

    def visit(step_index, inner):
        run_max, run_sum, run_acc = inner
        key_ids = lax.dynamic_index_in_dim(block_order, step_index, 1, False)
        key_blk = lax.dynamic_index_in_dim(key_piece, step_index, 1, False)
        value_blk = lax.dynamic_index_in_dim(value_piece, step_index, 1, False)
        member = 0
        key_pos = key_ids[member] * span + offsets
        operands = (run_max[member], run_sum[member], run_acc[member])

        def update(current, member=member, key_pos=key_pos):
            return online_update(
                current,
                queries[member],
                query_pos[member],
                key_blk[member],
                value_blk[member],
                key_pos,
                head_count,
            )

        result = update(operands)
        maxes = [result[0]]
        sums = [result[1]]
        accs = [result[2]]
        return (jnp.stack(maxes), jnp.stack(sums), jnp.stack(accs))

    run_max, run_sum, run_acc = lax.fori_loop(0, key_piece.shape[1], visit, initial)
    attention = (run_acc / jnp.transpose(run_sum, (0, 2, 1))[..., None]).astype(bf16)
    log_total = run_max + jnp.log(run_sum)
    attn_flat = attention.reshape(seq_count, 2, span, local_width)
    attn_part = jnp.einsum("spce,ed->spcd", attn_flat, full_out, preferred_element_type=f32)
    resid_mid = x_float + sum_rows(attn_part)
    full_gate_up, full_down, full_gain_mlp = (
        lax.all_gather(w_gate_up, ("dp", "ctx"), axis=0, tiled=True),
        lax.all_gather(w_down, ("dp", "ctx"), axis=1, tiled=True),
        lax.all_gather(gain_mlp, ("dp", "ctx"), axis=0, tiled=True),
    )
    rms_mlp = lax.rsqrt(jnp.mean(resid_mid * resid_mid, -1, keepdims=True) + EPSILON)
    unit_mlp = resid_mid * rms_mlp
    normed_mlp = (unit_mlp * full_gain_mlp.astype(f32)).astype(bf16)
    normed_mlp_full = gather_rows(normed_mlp)
    gate_up = jnp.einsum(
        "spcd,dtf->spctf", normed_mlp_full, full_gate_up, preferred_element_type=f32
    )
    gate = gate_up[:, :, :, 0]
    upper = gate_up[:, :, :, 1]
    sigma = jax.nn.sigmoid(gate)
    hidden = (gate * sigma * upper).astype(bf16)
    down_part = jnp.einsum("spcf,fd->spcd", hidden, full_down, preferred_element_type=f32)
    resid_out = resid_mid + sum_rows(down_part)
    block_output = resid_out.astype(bf16)
    back_gate_up, back_down, back_gain_mlp = (full_gate_up, full_down, full_gain_mlp)
    back_qkv, back_out, back_gain_attn = (full_qkv, full_out, full_gain_attn)
    cotan_full = gather_cotangent(cotangent)
    grad_down_local = jnp.einsum("spcf,spcd->fd", hidden, cotan_full, preferred_element_type=f32)
    grad_hidden = jnp.einsum("spcd,fd->spcf", cotan_full, back_down, preferred_element_type=f32)
    act_grad = jnp.stack(
        [grad_hidden * upper * sigma * (1.0 + gate * (1.0 - sigma)), grad_hidden * gate * sigma],
        axis=3,
    ).astype(bf16)
    grad_gate_up_local = jnp.einsum(
        "spcd,spctf->dtf", normed_mlp_full, act_grad, preferred_element_type=f32
    )
    grad_normed_mlp = sum_normed(
        jnp.einsum("spctf,dtf->spcd", act_grad, back_gate_up, preferred_element_type=f32)
    )
    gain_term_mlp = jnp.sum(grad_normed_mlp * unit_mlp, axis=(0, 1, 2))
    scaled_two = grad_normed_mlp * back_gain_mlp.astype(f32)
    grad_mid = cotangent.astype(f32) + rms_mlp * (
        scaled_two - unit_mlp * jnp.mean(scaled_two * unit_mlp, -1, keepdims=True)
    )
    mlp_shares = (
        lax.psum_scatter(
            grad_gate_up_local.astype(jnp.bfloat16), ("dp", "ctx"), scatter_dimension=0, tiled=True
        ).astype(jnp.float32),
        lax.psum_scatter(
            grad_down_local.astype(jnp.bfloat16), ("dp", "ctx"), scatter_dimension=1, tiled=True
        ).astype(jnp.float32),
        lax.psum_scatter(
            gain_term_mlp.astype(jnp.bfloat16), ("dp", "ctx"), scatter_dimension=0, tiled=True
        ).astype(jnp.float32),
    )
    grad_mid_b = grad_mid.astype(bf16)
    mid_full = gather_cotangent(grad_mid_b)
    grad_out_local = jnp.einsum("spce,spcd->ed", attn_flat, mid_full, preferred_element_type=f32)
    grad_attention = jnp.einsum(
        "spcd,ed->spce", mid_full, back_out, preferred_element_type=f32
    ).astype(bf16)
    grad_attention = grad_attention.reshape(seq_count, query_rows, head_count, HEAD_DIM)
    delta = jnp.transpose(
        jnp.sum(grad_attention.astype(f32) * attention.astype(f32), -1), (0, 2, 1)
    )
    all_keys, all_values = (
        lax.all_gather(key_send, "ctx", axis=1, tiled=True),
        lax.all_gather(value_send, "ctx", axis=1, tiled=True),
    )

    def back_step(grad_queries, slot):
        key_ids = lax.dynamic_index_in_dim(block_order, slot, 1, False)
        key_blk = lax.dynamic_index_in_dim(all_keys, slot, 1, False)
        value_blk = lax.dynamic_index_in_dim(all_values, slot, 1, False)
        member = 0
        key_pos = key_ids[member] * span + offsets

        def work(current, member=member, key_pos=key_pos):
            grad_query, grad_key, grad_value = backward_block(
                queries[member],
                query_pos[member],
                grad_attention[member],
                log_total[member],
                delta[member],
                key_blk[member],
                value_blk[member],
                key_pos,
                head_count,
            )
            return (current + grad_query, grad_key, grad_value)

        result = work(grad_queries[member])
        query_list = [result[0]]
        key_list = [result[1]]
        value_list = [result[2]]
        return (jnp.stack(query_list), (jnp.stack(key_list), jnp.stack(value_list)))

    start_grads = jnp.zeros((seq_count, query_rows, head_count, HEAD_DIM), f32)
    grad_queries, (key_terms, value_terms) = lax.scan(
        back_step, start_grads, jnp.arange(block_total, dtype=jnp.int32)
    )
    grad_keys, grad_values = (
        lax.psum_scatter(
            key_terms.astype(jnp.bfloat16), "ctx", scatter_dimension=0, tiled=True
        ).astype(jnp.float32),
        lax.psum_scatter(
            value_terms.astype(jnp.bfloat16), "ctx", scatter_dimension=0, tiled=True
        ).astype(jnp.float32),
    )
    grad_keys = jnp.transpose(grad_keys, (1, 0, 2, 3)).reshape(
        seq_count, query_rows, head_count, HEAD_DIM
    )
    grad_values = jnp.transpose(grad_values, (1, 0, 2, 3)).reshape(
        seq_count, query_rows, head_count, HEAD_DIM
    )
    qkv_grad = jnp.stack(
        [
            rope_back(grad_queries, cosine, sine) * 0.125,
            rope_back(grad_keys, cosine, sine),
            grad_values,
        ],
        axis=2,
    ).astype(bf16)
    qkv_grad = qkv_grad.reshape(seq_count, 2, span, 3, local_width)
    grad_qkv_local = jnp.einsum(
        "spcd,spcte->dte", normed_attn_full, qkv_grad, preferred_element_type=f32
    )
    grad_normed_attn = sum_normed(
        jnp.einsum("spcte,dte->spcd", qkv_grad, back_qkv, preferred_element_type=f32)
    )
    gain_term_attn = jnp.sum(grad_normed_attn * unit_attn, axis=(0, 1, 2))
    scaled_one = grad_normed_attn * back_gain_attn.astype(f32)
    input_grad = grad_mid + rms_attn * (
        scaled_one - unit_attn * jnp.mean(scaled_one * unit_attn, -1, keepdims=True)
    )
    shard_qkv, shard_out, shard_gain_attn = (
        lax.psum_scatter(
            grad_qkv_local.astype(jnp.bfloat16), ("dp", "ctx"), scatter_dimension=0, tiled=True
        ).astype(jnp.float32),
        lax.psum_scatter(
            grad_out_local.astype(jnp.bfloat16), ("dp", "ctx"), scatter_dimension=1, tiled=True
        ).astype(jnp.float32),
        lax.psum_scatter(
            gain_term_attn.astype(jnp.bfloat16), ("dp", "ctx"), scatter_dimension=0, tiled=True
        ).astype(jnp.float32),
    )
    shard_gate_up, shard_down, shard_gain_mlp = mlp_shares
    total_gain_attn, total_gain_mlp = lax.psum((shard_gain_attn, shard_gain_mlp), "tp")
    return (
        block_output,
        input_grad,
        shard_qkv,
        shard_out,
        total_gain_attn,
        shard_gate_up,
        shard_down,
        total_gain_mlp,
    )


def solution(mesh):
    in_specs = (
        P("dp", "ctx", "tp", None),
        P("dp", None),
        P(("dp", "ctx"), None, "tp"),
        P("tp", ("dp", "ctx")),
        P(("dp", "ctx")),
        P(("dp", "ctx"), None, "tp"),
        P("tp", ("dp", "ctx")),
        P(("dp", "ctx")),
        P("dp", "ctx", "tp", None),
    )
    out_specs = (
        P("dp", "ctx", "tp", None),
        P("dp", "ctx", "tp", None),
        P(("dp", "ctx"), None, "tp"),
        P("tp", ("dp", "ctx")),
        P(("dp", "ctx")),
        P(("dp", "ctx"), None, "tp"),
        P("tp", ("dp", "ctx")),
        P(("dp", "ctx")),
    )
    return jax.shard_map(body, mesh=mesh, in_specs=in_specs, out_specs=out_specs, check_vma=False)
```

profile of v0, /device:TPU:0, one launch (start us, length us, event | category | flops | bytes accessed | tf_op | source)
XLA Modules:
  0.0 1424.0 jit_solution(8658560242486038990)
XLA Ops:
  8.6 10.4 all-gather
  27.8 30.2 %all-gather.15.cloned.1.call-done = bf16[2048,3,512]{2,0,1:T(8,128)(2,1)} async-done(((bf16[256,3,512]{2,0,1:T(8,128)(2,1)}), bf16[2048,3,512]{2,0,1:T(8,128)(2,1)}) %all-gather.15.cloned.1.call-update) | async-done | bytes 6291472 | tf_op jit(solution)/shard_map/all_gather | solution.py:113
  58.0 8.8 copy.74
  66.9 39.0 %all-gather.13.cloned.1.call-done = bf16[1,2,256,2048]{3,2,1,0:T(8,128)(2,1)} async-done(((bf16[1,2,64,2048]{3,2,1,0:T(8,128)(2,1)}), bf16[1,2,256,2048]{3,2,1,0:T(8,128)(2,1)}) %all-gather.13.cloned.1.call-update) | async-done | bytes 2097168 | tf_op jit(solution)/shard_map/all_gather | solution.py:40
  105.9 6.2 convolution_bitcast_fusion.2
  121.6 3.9 add_convert_fusion.1
  133.6 15.4 %all-gather.17.cloned.1.call-done = bf16[1,8,256,512]{3,2,0,1:T(8,128)(2,1)} async-done(((bf16[1,2,256,512]{3,2,0,1:T(8,128)(2,1)}), bf16[1,8,256,512]{3,2,0,1:T(8,128)(2,1)}) %all-gather.17.cloned.1.call-update) | async-done | bytes 2097168 | tf_op jit(solution)/shard_map/all_gather | solution.py:134
  149.0 3.9 copy.77
  152.9 20.7 %all-gather.19.cloned.1.call-done = bf16[1,8,256,512]{3,2,0,1:T(8,128)(2,1)} async-done(((bf16[1,2,256,512]{3,2,0,1:T(8,128)(2,1)}), bf16[1,8,256,512]{3,2,0,1:T(8,128)(2,1)}) %all-gather.19.cloned.1.call-update) | async-done | bytes 2097168 | tf_op jit(solution)/shard_map/all_gather | solution.py:135
  173.6 3.9 copy.78
  177.6 92.5 %while.34 = (s32[]{:T(128)}, f32[1,8,512]{2,1,0:T(8,128)S(1)}, f32[1,8,512]{2,1,0:T(8,128)S(1)}, f32[1,512,8,64]{1,3,2,0:T(8,128)S(1)}, s32[1,8]{1,0:T(1,128)S(1...) while((s32[]{:T(128)}, f32[1,8,512]{2,1,0:T(8,128)S(1)}, ...), condition=%wide.region_4.5_spmd.clone, body=%wide.region_1.4_spmd.clone.sunk | while | flops 947548928 | bytes 34334904 | solution.py:163
  183.0 3.1 fusion.167
  194.6 3.1 fusion.167
  206.1 3.1 fusion.167
  217.7 3.1 fusion.167
  270.4 5.1 convolution_bitcast_fusion.1
  276.1 8.9 all-gather.1
  285.1 67.6 %reduce-scatter.11.cloned.1.call-done = f32[1,2,64,2048]{3,2,1,0:T(8,128)} async-done(((f32[1,2,256,2048]{3,2,1,0:T(8,128)}), f32[1,2,64,2048]{3,2,1,0:T(8,128)}) %reduce-scatter.11.cloned.1.call-update) | async-done | bytes 1048592 | tf_op jit(solution)/shard_map/reduce_scatter | solution.py:44
  355.4 3.8 copy.80
  361.0 40.7 %all-gather.23.cloned.1.call-done = bf16[1,2,256,2048]{3,2,1,0:T(8,128)(2,1)} async-done(((bf16[1,2,64,2048]{3,2,1,0:T(8,128)(2,1)}), bf16[1,2,256,2048]{3,2,1,0:T(8,128)(2,1)}) %all-gather.23.cloned.1.call-update) | async-done | bytes 2097168 | tf_op jit(solution)/shard_map/all_gather | solution.py:40
  401.7 91.0 %all-gather.25.cloned.1.call-done = bf16[2048,2,2048]{2,0,1:T(8,128)(2,1)} async-done(((bf16[256,2,2048]{2,0,1:T(8,128)(2,1)}), bf16[2048,2,2048]{2,0,1:T(8,128)(2,1)}) %all-gather.25.cloned.1.call-update) | async-done | bytes 16777232 | tf_op jit(solution)/shard_map/all_gather | solution.py:170
  492.7 15.1 %fusion.48 = f32[1,2,256,2,2048]{4,2,3,1,0:T(8,128)} fusion(bf16[2048,2,2048]{2,0,1:T(8,128)(2,1)} %all-gather.25.cloned.1.call-done, bf16[1,2,256,2048]{3,2,1,0:T(8,128)(2,1)} %all-gather.23.cloned.1.call-done), kind=kOutput, calls=%fused_computation.71 | convolution fusion | flops 8589934592 | bytes 27262976 | tf_op jit(solution)/shard_map/spcd,dtf->spctf/dot_general | solution.py:178
  507.8 32.2 %all-gather.29.cloned.1.call-done = bf16[1,2,256,2048]{3,2,1,0:T(8,128)(2,1)} async-done(((bf16[1,2,64,2048]{3,2,1,0:T(8,128)(2,1)}), bf16[1,2,256,2048]{3,2,1,0:T(8,128)(2,1)}) %all-gather.29.cloned.1.call-update) | async-done | bytes 2097168 | tf_op jit(solution)/shard_map/all_gather | solution.py:48
  540.0 56.4 %all-gather.27.cloned.1.call-done = bf16[2048,2048]{1,0:T(8,128)(2,1)} async-done(((bf16[2048,256]{1,0:T(8,128)(2,1)}), bf16[2048,2048]{1,0:T(8,128)(2,1)}) %all-gather.27.cloned.1.call-update) | async-done | bytes 8388624 | tf_op jit(solution)/shard_map/all_gather | solution.py:171
  596.4 11.2 fusion.71
  609.8 13.8 fusion.54
  623.6 76.9 %reduce-scatter.15.cloned.1.call-done = f32[1,2,64,2048]{3,2,1,0:T(8,128)} async-done(((f32[1,2,256,2048]{3,2,1,0:T(8,128)}), f32[1,2,64,2048]{3,2,1,0:T(8,128)}) %reduce-scatter.15.cloned.1.call-update) | async-done | bytes 1048592 | tf_op jit(solution)/shard_map/reduce_scatter | solution.py:52
  704.7 46.0 %all-gather.31.cloned.1.call-done = bf16[1,2,256,2048]{3,2,1,0:T(8,128)(2,1)} async-done(((bf16[1,2,64,2048]{3,2,1,0:T(8,128)(2,1)}), bf16[1,2,256,2048]{3,2,1,0:T(8,128)(2,1)}) %all-gather.31.cloned.1.call-update) | async-done | bytes 2097168 | tf_op jit(solution)/shard_map/all_gather | solution.py:48
  750.8 3.5 fusion.76
  760.7 122.6 %while.35 = (s32[]{:T(128)}, f32[1,512,8,64]{1,3,2,0:T(8,128)}, bf16[8,1,256,512]{3,2,0,1:T(8,128)(2,1)}, bf16[8,1,256,512]{3,2,0,1:T(8,128)(2,1)}, s32[8]{0:T(1...) while((s32[]{:T(128)}, f32[1,512,8,64]{1,3,2,0:T(8,128)}, ...), condition=%wide.wide.region_12.13_spmd.clone, body=%wide.wide.region_11.12_spmd.clone.sunk | while | flops 679871232 | bytes 27977976 | solution.py:262
  884.8 8.4 bitcast_convert_fusion.1
  894.3 4.2 bitcast_convert_fusion.3
  900.3 13.1 reduce-scatter.17.cloned.1.call-done
  927.3 20.3 %reduce-scatter.19.cloned.1.call-done = bf16[2,1,256,512]{3,2,0,1:T(8,128)(2,1)} async-done(((bf16[8,1,256,512]{3,2,0,1:T(8,128)(2,1)}), bf16[2,1,256,512]{3,2,0,1:T(8,128)(2,1)}) %reduce-scatter.19.cloned.1.call-update) | async-done | bytes 524304 | tf_op jit(solution)/shard_map/reduce_scatter | solution.py:269
  947.6 8.6 fusion.51
  957.8 11.1 fusion.57
  970.7 6.4 bitcast_convert_fusion.2
  978.7 14.6 %bitcast_convert_fusion = bf16[2048,2,2048]{2,0,1:T(8,128)(2,1)} fusion(bf16[2,256,1,2048]{3,1,0,2:T(8,128)(2,1)} %copy-done.35, bf16[2,256,1,2048]{3,1,0,2:T(8,128)(2,1)} %copy-done.34, bf16[1,2,256,2048]{3,2,1,0:T(8,128)(2,1)S(1)} %copy-done.28), kind=kOutput, calls=%fused_computation.58 | convolution fusion | flops 8606711808 | bytes 23068672 | tf_op jit(solution)/shard_map/spcd,spctf->dtf/dot_general | solution.py:197
  995.2 27.0 %reduce-scatter.29.cloned.1.call-done = bf16[2048,256]{1,0:T(8,128)(2,1)} async-done(((bf16[2048,2048]{1,0:T(8,128)(2,1)}), bf16[2048,256]{1,0:T(8,128)(2,1)}) %reduce-scatter.29.cloned.1.call-update) | async-done | bytes 1048592 | tf_op jit(solution)/shard_map/reduce_scatter | solution.py:212
  1024.9 41.6 %reduce-scatter.25.cloned.1.call-done = bf16[512,256]{1,0:T(8,128)(2,1)} async-done(((bf16[512,2048]{1,0:T(8,128)(2,1)}), bf16[512,256]{1,0:T(8,128)(2,1)}) %reduce-scatter.25.cloned.1.call-update) | async-done | bytes 262160 | tf_op jit(solution)/shard_map/reduce_scatter | solution.py:303
  1068.3 77.8 %reduce-scatter.21.cloned.1.call-done = f32[1,2,64,2048]{3,2,1,0:T(8,128)} async-done(((f32[1,2,256,2048]{3,2,1,0:T(8,128)}), f32[1,2,64,2048]{3,2,1,0:T(8,128)}) %reduce-scatter.21.cloned.1.call-update) | async-done | bytes 1048592 | tf_op jit(solution)/shard_map/reduce_scatter | solution.py:52
  1147.7 13.6 all-reduce.3
  1161.4 12.5 all-reduce.2
  1173.9 51.9 %reduce-scatter.13.cloned.1.call-done = f32[1,2,64,2048]{3,2,1,0:T(8,128)} async-done(((f32[1,2,256,2048]{3,2,1,0:T(8,128)}), f32[1,2,64,2048]{3,2,1,0:T(8,128)}) %reduce-scatter.13.cloned.1.call-update) | async-done | bytes 1048592 | tf_op jit(solution)/shard_map/reduce_scatter | solution.py:44
  1225.8 3.1 fusion.85
  1228.9 62.4 %reduce-scatter.23.cloned.1.call-done = bf16[256,3,512]{2,0,1:T(8,128)(2,1)} async-done(((bf16[2048,3,512]{2,0,1:T(8,128)(2,1)}), bf16[256,3,512]{2,0,1:T(8,128)(2,1)}) %reduce-scatter.23.cloned.1.call-update) | async-done | bytes 786448 | tf_op jit(solution)/shard_map/reduce_scatter | solution.py:300
  1293.8 117.1 %reduce-scatter.27.cloned.1.call-done = bf16[256,2,2048]{2,0,1:T(8,128)(2,1)} async-done(((bf16[2048,2,2048]{2,0,1:T(8,128)(2,1)}), bf16[256,2,2048]{2,0,1:T(8,128)(2,1)}) %reduce-scatter.27.cloned.1.call-update) | async-done | bytes 2097168 | tf_op jit(solution)/shard_map/reduce_scatter | solution.py:209
  1410.9 5.8 copy.97
  (411 shorter events, 267.6 us)
Async XLA Ops:
  7.2 50.9 %all-gather.15.cloned.1.call-start = ((), (), s32[]{:S(2)}) async-start(), calls=%async_computation.11 | async-start | bytes 7077888 | tf_op jit(solution)/shard_map/all_gather | solution.py:113
  7.9 98.0 %all-gather.13.cloned.1.call-start = ((), (), s32[]{:S(2)}) async-start(), calls=%async_computation.10 | async-start | bytes 2621440 | tf_op jit(solution)/shard_map/all_gather | solution.py:40
  23.0 126.0 %all-gather.17.cloned.1.call-start = ((), (), s32[]{:S(2)}) async-start(), calls=%async_computation.12 | async-start | bytes 2621440 | tf_op jit(solution)/shard_map/all_gather | solution.py:134
  24.3 107.7 %copy-start.11 = (f32[512,64]{0,1:T(8,128)}, f32[512,64]{0,1:T(8,128)S(1)}, u32[]{:S(2)}) copy-start(f32[512,64]{0,1:T(8,128)S(1)} %get-tuple-element.492) | copy-start | bytes 393220
  24.3 107.7 %copy-start.15 = (f32[512,64]{0,1:T(8,128)}, f32[512,64]{0,1:T(8,128)S(1)}, u32[]{:S(2)}) copy-start(f32[512,64]{0,1:T(8,128)S(1)} %get-tuple-element.491) | copy-start | bytes 393220
  26.2 40.7 %copy-start.5 = (f32[512,8,64]{0,2,1:T(8,128)}, f32[512,8,64]{0,2,1:T(8,128)S(1)}, u32[]{:S(2)}) copy-start(f32[512,8,64]{0,2,1:T(8,128)S(1)} %mul.365) | copy-start | bytes 3145732
  112.1 15.4 %copy-start.10 = (f32[1,512,3,8,64]{1,4,3,2,0:T(8,128)}, f32[1,512,3,8,64]{1,4,3,2,0:T(8,128)S(1)}, u32[]{:S(2)}) copy-start(f32[1,512,3,8,64]{1,4,3,2,0:T(8,128)S(1)} %convolution_bitcast_fusion.2) | copy-start | bytes 9437188
  127.5 46.1 %all-gather.19.cloned.1.call-start = ((), (), s32[]{:S(2)}) async-start(), calls=%async_computation.13 | async-start | bytes 2621440 | tf_op jit(solution)/shard_map/all_gather | solution.py:135
  128.4 3.6 copy-start.19
  128.4 3.6 copy-start.20
  131.1 139.3 %all-gather.21.cloned.1.call-start = ((), (), s32[]{:S(2)}) async-start(), calls=%async_computation.14 | async-start | bytes 2359296 | tf_op jit(solution)/shard_map/all_gather | solution.py:114
  131.7 221.0 %reduce-scatter.11.cloned.1.call-start = ((), (), s32[]{:S(2)}) async-start(), calls=%async_computation.15 | async-start | bytes 5242880 | tf_op jit(solution)/shard_map/reduce_scatter | solution.py:44
  152.9 24.7 %copy-start.31 = (s32[1,8]{1,0:T(1,128)S(1)}, s32[1,8]{1,0:T(1,128)}, u32[]{:S(2)}) copy-start(s32[1,8]{1,0:T(1,128)} %param.14) | copy-start | bytes 100
  183.0 3.5 copy-start
  194.6 3.4 copy-start
  206.1 3.4 copy-start
  217.7 3.4 copy-start
  252.3 3.4 copy-start
  263.9 3.4 copy-start
  270.4 5.1 copy-start.17
  275.5 77.2 %copy-start.3 = (bf16[1,2,64,2048]{3,2,1,0:T(8,128)(2,1)S(1)}, bf16[1,2,64,2048]{3,2,1,0:T(8,128)(2,1)}, u32[]{:S(2)}) copy-start(bf16[1,2,64,2048]{3,2,1,0:T(8,128)(2,1)} %param.13) | copy-start | bytes 1572868
  275.5 126.2 %all-gather.23.cloned.1.call-start = ((), (), s32[]{:S(2)}) async-start(), calls=%async_computation.16 | async-start | bytes 2621440 | tf_op jit(solution)/shard_map/all_gather | solution.py:40
  354.2 347.9 %copy-start.1 = (f32[1,2,64,2048]{3,2,1,0:T(8,128)}, f32[1,2,64,2048]{3,2,1,0:T(8,128)S(1)}, u32[]{:S(2)}) copy-start(f32[1,2,64,2048]{3,2,1,0:T(8,128)S(1)} %get-tuple-element.460) | copy-start | bytes 3145732
  355.4 137.4 %all-gather.25.cloned.1.call-start = ((), (), s32[]{:S(2)}) async-start(), calls=%async_computation.17 | async-start | bytes 18874368 | tf_op jit(solution)/shard_map/all_gather | solution.py:170
  359.2 180.8 %all-gather.29.cloned.1.call-start = ((), (), s32[]{:S(2)}) async-start(), calls=%async_computation.20 | async-start | bytes 2621440 | tf_op jit(solution)/shard_map/all_gather | solution.py:48
  360.0 236.4 %all-gather.27.cloned.1.call-start = ((), (), s32[]{:S(2)}) async-start(), calls=%async_computation.18 | async-start | bytes 9437184 | tf_op jit(solution)/shard_map/all_gather | solution.py:171
  360.6 339.9 %reduce-scatter.15.cloned.1.call-start = ((), (), s32[]{:S(2)}) async-start(), calls=%async_computation.21 | async-start | bytes 5242880 | tf_op jit(solution)/shard_map/reduce_scatter | solution.py:52
  623.5 78.6 %copy-start.8 = (bf16[1,2,64,2048]{3,2,1,0:T(8,128)(2,1)S(1)}, bf16[1,2,64,2048]{3,2,1,0:T(8,128)(2,1)}, u32[]{:S(2)}) copy-start(bf16[1,2,64,2048]{3,2,1,0:T(8,128)(2,1)} %param.21) | copy-start | bytes 1572868
  623.6 127.2 %all-gather.31.cloned.1.call-start = ((), (), s32[]{:S(2)}) async-start(), calls=%async_computation.22 | async-start | bytes 2621440 | tf_op jit(solution)/shard_map/all_gather | solution.py:48
  704.5 208.9 %reduce-scatter.17.cloned.1.call-start = ((), (), s32[]{:S(2)}) async-start(), calls=%async_computation.23 | async-start | bytes 2621440 | tf_op jit(solution)/shard_map/reduce_scatter | solution.py:266
  755.9 4.8 copy-start.13
  883.3 64.3 %reduce-scatter.19.cloned.1.call-start = ((), (), s32[]{:S(2)}) async-start(), calls=%async_computation.24 | async-start | bytes 2621440 | tf_op jit(solution)/shard_map/reduce_scatter | solution.py:269
  883.9 138.4 %reduce-scatter.29.cloned.1.call-start = ((), (), s32[]{:S(2)}) async-start(), calls=%async_computation.29 | async-start | bytes 9437184 | tf_op jit(solution)/shard_map/reduce_scatter | solution.py:212
  893.3 5.5 copy-start.6
  893.3 173.2 %reduce-scatter.25.cloned.1.call-start = ((), (), s32[]{:S(2)}) async-start(), calls=%async_computation.27 | async-start | bytes 2359296 | tf_op jit(solution)/shard_map/reduce_scatter | solution.py:303
  898.5 247.6 %reduce-scatter.21.cloned.1.call-start = ((), (), s32[]{:S(2)}) async-start(), calls=%async_computation.25 | async-start | bytes 5242880 | tf_op jit(solution)/shard_map/reduce_scatter | solution.py:52
  899.4 16.1 %copy-start.12 = (f32[512,64]{0,1:T(8,128)S(1)}, f32[512,64]{0,1:T(8,128)}, u32[]{:S(2)}) copy-start(f32[512,64]{0,1:T(8,128)} %copy-done.11) | copy-start | bytes 393220
  919.7 6.4 copy-start.14
  926.2 21.4 %copy-start.21 = (bf16[2,256,1,512]{3,1,2,0:T(8,128)(2,1)S(1)}, bf16[2,256,1,512]{3,1,2,0:T(8,128)(2,1)}, u32[]{:S(2)}) copy-start(bf16[2,256,1,512]{3,1,2,0:T(8,128)(2,1)} %copy.91) | copy-start | bytes 1572868
  956.2 269.6 %reduce-scatter.13.cloned.1.call-start = ((), (), s32[]{:S(2)}) async-start(), calls=%async_computation.19 | async-start | bytes 5242880 | tf_op jit(solution)/shard_map/reduce_scatter | solution.py:44
  969.0 322.3 %reduce-scatter.23.cloned.1.call-start = ((), (), s32[]{:S(2)}) async-start(), calls=%async_computation.26 | async-start | bytes 7077888 | tf_op jit(solution)/shard_map/reduce_scatter | solution.py:300
  977.1 433.8 %reduce-scatter.27.cloned.1.call-start = ((), (), s32[]{:S(2)}) async-start(), calls=%async_computation.28 | async-start | bytes 18874368 | tf_op jit(solution)/shard_map/reduce_scatter | solution.py:209
  993.3 152.7 %copy-start.4 = (bf16[1,2,64,2048]{3,2,1,0:T(8,128)(2,1)S(1)}, bf16[1,2,64,2048]{3,2,1,0:T(8,128)(2,1)}, u32[]{:S(2)}) copy-start(bf16[1,2,64,2048]{3,2,1,0:T(8,128)(2,1)} %param.13) | copy-start | bytes 1572868
  993.3 152.7 %copy-start.24 = (f32[8,1,256]{2,1,0:T(1,128)S(1)}, f32[8,1,256]{2,1,0:T(1,128)}, u32[]{:S(2)}) copy-start(f32[8,1,256]{2,1,0:T(1,128)} %copy-done.23) | copy-start | bytes 24580
  993.3 152.7 %copy-start.26 = (f32[2,64]{1,0:T(2,128)S(1)}, f32[2,64]{1,0:T(2,128)}, u32[]{:S(2)}) copy-start(f32[2,64]{1,0:T(2,128)} %copy-done.25) | copy-start | bytes 1540
  993.4 232.4 %copy-start.2 = (f32[1,2,64,2048]{3,2,1,0:T(8,128)S(1)}, f32[1,2,64,2048]{3,2,1,0:T(8,128)}, u32[]{:S(2)}) copy-start(f32[1,2,64,2048]{3,2,1,0:T(8,128)} %copy-done.1) | copy-start | bytes 3145732
  993.4 232.4 %copy-start.7 = (f32[1,2,64,2048]{3,2,1,0:T(8,128)S(1)}, f32[1,2,64,2048]{3,2,1,0:T(8,128)}, u32[]{:S(2)}) copy-start(f32[1,2,64,2048]{3,2,1,0:T(8,128)} %reduce-scatter.15.cloned.1.call-done) | copy-start | bytes 3145732
  993.4 232.4 %copy-start.9 = (bf16[1,2,64,2048]{3,2,1,0:T(8,128)(2,1)S(1)}, bf16[1,2,64,2048]{3,2,1,0:T(8,128)(2,1)}, u32[]{:S(2)}) copy-start(bf16[1,2,64,2048]{3,2,1,0:T(8,128)(2,1)} %param.21) | copy-start | bytes 1572868
  (15 other events, 25.1 us)
Sparse Core Ops, SparseCore 0:
  9.9 48.1 all-gather.14
  60.2 45.6 all-gather.12
  127.6 21.3 all-gather.16
  151.0 22.5 all-gather.18
  175.3 28.0 all-gather.20
  275.6 77.0 reduce-scatter.10
  355.5 46.1 all-gather.22
  404.2 88.5 all-gather.24
  494.3 45.6 all-gather.28
  541.7 54.6 all-gather.26
  623.7 76.7 reduce-scatter.14
  704.6 46.1 all-gather.30
  883.4 29.9 reduce-scatter.16
  916.4 31.1 reduce-scatter.18
  950.9 71.2 reduce-scatter.28
  1025.3 41.1 reduce-scatter.24
  1069.2 76.7 reduce-scatter.20
  1148.2 77.5 reduce-scatter.12
  1229.2 62.0 reduce-scatter.22
  1294.7 116.1 reduce-scatter.26
where the time goes:
time: 1430 us; the launch traced here: 1420 us
  waiting for transfers between devices  931 us (65%)
  matrix products  222 us (16%)
  local copies, waits for them, and re-layouts  109 us (8%)
  other arithmetic  85.4 us (6%)
  blocking collectives  45.4 us (3%)
  between operations  16 us (1%)
    reduce_scatter x2, waiting for transfers between devices, sum_normed(): return lax.psum_scatter(values, 'tp', scatter_dimension=2, tiled=True)  155 us
    reduce_scatter x2, waiting for transfers between devices, sum_rows(): return lax.psum_scatter(values, 'tp', scatter_dimension=2, tiled=True)  119 us
    reduce_scatter x1, waiting for transfers between devices, body(): lax.psum_scatter(grad_gate_up_local.astype(jnp.bfloat16), ('dp', 'ctx'),...  117 us
    all_gather x1, waiting for transfers between devices, body(): lax.all_gather(w_gate_up, ('dp', 'ctx'), axis=0, tiled=True)  91 us
    all_gather x2, waiting for transfers between devices, gather_rows(): return lax.all_gather(values, 'tp', axis=2, tiled=True)  79.7 us
    all_gather x2, waiting for transfers between devices, gather_cotangent(): return lax.all_gather(values, 'tp', axis=2, tiled=True)  78.2 us
    reduce_scatter x1, waiting for transfers between devices, body(): lax.psum_scatter(grad_qkv_local.astype(jnp.bfloat16), ('dp', 'ctx'), scat...  62.4 us
    all_gather x1, waiting for transfers between devices, body(): lax.all_gather(w_down, ('dp', 'ctx'), axis=1, tiled=True)  56.4 us
  transfers between devices with their start and end apart: 20, of which 19 were waited for; matrix products, arithmetic and copies ran while one was open for 15% of the time, Pallas kernels for 0%

commit v1 on v0

--- a/solution.py
+++ b/solution.py
@@ -7,6 +7,22 @@
 EPSILON = 1e-05
 ROPE_BASE = 130000.0
 NEG_LARGE = -1e30
+
+
+def gather_around(x, axis, dim):
+    ways, here, step = (lax.axis_size(axis), lax.axis_index(axis), x.shape[dim])
+    dims = [n * ways if d == dim else n for d, n in enumerate(x.shape)]
+    full = lax.dynamic_update_slice_in_dim(jnp.zeros(dims, x.dtype), x, here * step, axis=dim)
+    going_up = going_down = x
+    for far in range(1, ways // 2 + 1):
+        going_up = lax.ppermute(going_up, axis, [(d, (d + 1) % ways) for d in range(ways)])
+        full = lax.dynamic_update_slice_in_dim(full, going_up, (here - far) % ways * step, axis=dim)
+        if 2 * far < ways:
+            going_down = lax.ppermute(going_down, axis, [(d, (d - 1) % ways) for d in range(ways)])
+            full = lax.dynamic_update_slice_in_dim(
+                full, going_down, (here + far) % ways * step, axis=dim
+            )
+    return full
 
 
 def rope_tables(positions, head_size):
@@ -45,7 +61,7 @@
 
 
 def gather_cotangent(values):
-    return lax.all_gather(values, "tp", axis=2, tiled=True)
+    return gather_around(values, "tp", 2)
 
 
 def sum_normed(values):

time: 1430 us -> 1410 us (0.986)
  waiting for transfers between devices: 931 us -> 860 us
  starting transfers between devices: 2.07 us -> 39.1 us
    all_gather x2 -> x0, waiting for transfers between devices: 78.2 us -> none  [gather_cotangent(): return lax.all_gather(values, 'tp', axis=2, tiled=True)]
    ppermute x0 -> x6, waiting for transfers between devices: none -> 61.1 us  [the longest x4 56.2 us: gather_around(): lax.ppermute(going_up, axis, [(d, (d + 1) % ways) for d in range(ways)])]
    all_gather x2, waiting for transfers between devices: 79.7 us -> 41.1 us  [gather_rows(): return lax.all_gather(values, 'tp', axis=2, tiled=True)]
    ppermute x0 -> x6, starting transfers between devices: none -> 37.7 us  [the longest x4 33 us: gather_around(): lax.ppermute(going_up, axis, [(d, (d + 1) % ways) for d in range(ways)])]
    unnamed x80 -> x88, local copies, waits for them, and re-layouts: 29.5 us -> 33.4 us
  transfers between devices with their start and end apart: 20 -> 24, of which waited for: 19 -> 23; matrix products, arithmetic and copies ran while one was open for 15% -> 16% of each run, Pallas kernels for 0% -> 0%
where the time goes in v1:
time: 1410 us; the launch traced here: 1400 us
  waiting for transfers between devices  860 us (61%)
  matrix products  220 us (16%)
  local copies, waits for them, and re-layouts  121 us (9%)
  other arithmetic  83.8 us (6%)
  blocking collectives  45.4 us (3%)
  starting transfers between devices  39.1 us (3%)
  loops' own time  17.5 us (1%)
  between operations  15.9 us (1%)
    reduce_scatter x2, waiting for transfers between devices, sum_normed(): return lax.psum_scatter(values, 'tp', scatter_dimension=2, tiled=True)  155 us
    reduce_scatter x2, waiting for transfers between devices, sum_rows(): return lax.psum_scatter(values, 'tp', scatter_dimension=2, tiled=True)  119 us
    reduce_scatter x1, waiting for transfers between devices, body(): lax.psum_scatter(grad_gate_up_local.astype(jnp.bfloat16), ('dp', 'ctx'),...  117 us
    all_gather x1, waiting for transfers between devices, body(): lax.all_gather(w_gate_up, ('dp', 'ctx'), axis=0, tiled=True)  90.4 us
    reduce_scatter x1, waiting for transfers between devices, body(): lax.psum_scatter(grad_qkv_local.astype(jnp.bfloat16), ('dp', 'ctx'), scat...  62.2 us
    ppermute x4, waiting for transfers between devices, gather_around(): lax.ppermute(going_up, axis, [(d, (d + 1) % ways) for d in range(ways)])  56.2 us
    all_gather x1, waiting for transfers between devices, body(): lax.all_gather(w_down, ('dp', 'ctx'), axis=1, tiled=True)  42.8 us
    reduce_scatter x1, waiting for transfers between devices, body(): lax.psum_scatter(grad_out_local.astype(jnp.bfloat16), ('dp', 'ctx'), scat...  41.6 us
  transfers between devices with their start and end apart: 24, of which 23 were waited for; matrix products, arithmetic and copies ran while one was open for 16% of the time, Pallas kernels for 0%

profile of v1, /device:TPU:0, one launch (start us, length us, event | category | flops | bytes accessed | tf_op | source)
XLA Modules:
  0.0 1402.1 jit_solution(16046635889360990156)
XLA Ops:
  8.6 10.4 all-gather
  26.6 31.4 %all-gather.13.cloned.1.call-done = bf16[2048,3,512]{2,0,1:T(8,128)(2,1)} async-done(((bf16[256,3,512]{2,0,1:T(8,128)(2,1)}), bf16[2048,3,512]{2,0,1:T(8,128)(2,1)}) %all-gather.13.cloned.1.call-update) | async-done | bytes 6291472 | tf_op jit(solution)/shard_map/all_gather | solution.py:129
  58.0 8.8 copy.74
  66.9 39.0 %all-gather.11.cloned.1.call-done = bf16[1,2,256,2048]{3,2,1,0:T(8,128)(2,1)} async-done(((bf16[1,2,64,2048]{3,2,1,0:T(8,128)(2,1)}), bf16[1,2,256,2048]{3,2,1,0:T(8,128)(2,1)}) %all-gather.11.cloned.1.call-update) | async-done | bytes 2097168 | tf_op jit(solution)/shard_map/all_gather | solution.py:56
  105.9 6.2 convolution_bitcast_fusion.2
  127.8 16.1 %all-gather.15.cloned.1.call-done = bf16[1,8,256,512]{3,2,0,1:T(8,128)(2,1)} async-done(((bf16[1,2,256,512]{3,2,0,1:T(8,128)(2,1)}), bf16[1,8,256,512]{3,2,0,1:T(8,128)(2,1)}) %all-gather.15.cloned.1.call-update) | async-done | bytes 2097168 | tf_op jit(solution)/shard_map/all_gather | solution.py:150
  143.9 3.9 copy.77
  147.8 20.7 %all-gather.17.cloned.1.call-done = bf16[1,8,256,512]{3,2,0,1:T(8,128)(2,1)} async-done(((bf16[1,2,256,512]{3,2,0,1:T(8,128)(2,1)}), bf16[1,8,256,512]{3,2,0,1:T(8,128)(2,1)}) %all-gather.17.cloned.1.call-update) | async-done | bytes 2097168 | tf_op jit(solution)/shard_map/all_gather | solution.py:151
  168.5 3.9 copy.78
  172.5 92.6 %while.34 = (s32[]{:T(128)}, f32[1,8,512]{2,1,0:T(8,128)S(1)}, f32[1,8,512]{2,1,0:T(8,128)S(1)}, f32[1,512,8,64]{1,3,2,0:T(8,128)S(1)}, s32[1,8]{1,0:T(1,128)S(1...) while((s32[]{:T(128)}, f32[1,8,512]{2,1,0:T(8,128)S(1)}, ...), condition=%wide.region_4.5_spmd.clone, body=%wide.region_1.4_spmd.clone.sunk | while | flops 947548928 | bytes 34334904 | solution.py:179
  177.9 3.1 fusion.166
  189.5 3.1 fusion.166
  247.3 3.1 fusion.166
  265.4 5.1 convolution_bitcast_fusion.1
  271.2 8.9 all-gather.1
  280.1 67.6 %reduce-scatter.11.cloned.1.call-done = f32[1,2,64,2048]{3,2,1,0:T(8,128)} async-done(((f32[1,2,256,2048]{3,2,1,0:T(8,128)}), f32[1,2,64,2048]{3,2,1,0:T(8,128)}) %reduce-scatter.11.cloned.1.call-update) | async-done | bytes 1048592 | tf_op jit(solution)/shard_map/reduce_scatter | solution.py:60
  350.4 3.8 copy.80
  361.5 19.1 %collective-permute-done = bf16[1,2,64,2048]{3,2,1,0:T(8,128)(2,1)} collective-permute-done((bf16[1,2,64,2048]{3,2,1,0:T(8,128)(2,1)S(1)}, bf16[1,2,64,2048]{3,2,1,0:T(8,128)(2,1)}, u32[]{:S(2)}, u32[]{:S(2)}) %collective-permute-start) | collective-permute-done | bytes 524320 | tf_op jit(solution)/shard_map/ppermute | solution.py:18
  380.6 20.9 %collective-permute-start.2 = (bf16[1,2,64,2048]{3,2,1,0:T(8,128)(2,1)}, bf16[1,2,64,2048]{3,2,1,0:T(8,128)(2,1)S(1)}, u32[]{:S(2)}, u32[]{:S(2)}) collective-permute-start(bf16[1,2,64,2048]{3,2,1,0:T(8,128)(2,1)} %collective-permute-done), channel_id=1, source_target_pairs={{0,1},{1,2},{2,3},{3,0},{4,5},{5,6},{6,7},{7,4},{8,9},{9,10},{10,1... | collective-permute-start | bytes 1572872 | tf_op jit(solution)/shard_map/ppermute | solution.py:18
  403.5 3.8 collective-permute-done.1
  409.2 14.8 %collective-permute-done.2 = bf16[1,2,64,2048]{3,2,1,0:T(8,128)(2,1)S(1)} collective-permute-done((bf16[1,2,64,2048]{3,2,1,0:T(8,128)(2,1)}, bf16[1,2,64,2048]{3,2,1,0:T(8,128)(2,1)S(1)}, u32[]{:S(2)}, u32[]{:S(2)}) %collective-permute-start.2) | collective-permute-done | bytes 524320 | tf_op jit(solution)/shard_map/ppermute | solution.py:18
  427.0 90.4 %all-gather.23.cloned.1.call-done = bf16[2048,2,2048]{2,0,1:T(8,128)(2,1)} async-done(((bf16[256,2,2048]{2,0,1:T(8,128)(2,1)}), bf16[2048,2,2048]{2,0,1:T(8,128)(2,1)}) %all-gather.23.cloned.1.call-update) | async-done | bytes 16777232 | tf_op jit(solution)/shard_map/all_gather | solution.py:186
  517.4 15.0 %fusion.48 = f32[1,2,256,2,2048]{4,2,3,1,0:T(8,128)} fusion(bf16[2048,2,2048]{2,0,1:T(8,128)(2,1)} %all-gather.23.cloned.1.call-done, bf16[1,2,256,2048]{3,2,1,0:T(8,128)(2,1)} %all-gather.21.cloned.1.call-done), kind=kOutput, calls=%fused_computation.71 | convolution fusion | flops 8589934592 | bytes 27262976 | tf_op jit(solution)/shard_map/spcd,dtf->spctf/dot_general | solution.py:194
  532.3 42.8 %all-gather.25.cloned.1.call-done = bf16[2048,2048]{1,0:T(8,128)(2,1)} async-done(((bf16[2048,256]{1,0:T(8,128)(2,1)}), bf16[2048,2048]{1,0:T(8,128)(2,1)}) %all-gather.25.cloned.1.call-update) | async-done | bytes 8388624 | tf_op jit(solution)/shard_map/all_gather | solution.py:187
  575.2 11.3 fusion.67
  588.4 13.8 fusion.54
  602.2 76.9 %reduce-scatter.15.cloned.1.call-done = f32[1,2,64,2048]{3,2,1,0:T(8,128)} async-done(((f32[1,2,256,2048]{3,2,1,0:T(8,128)}), f32[1,2,64,2048]{3,2,1,0:T(8,128)}) %reduce-scatter.15.cloned.1.call-update) | async-done | bytes 1048592 | tf_op jit(solution)/shard_map/reduce_scatter | solution.py:68
  687.4 13.1 collective-permute-done.3
  700.5 9.1 collective-permute-start.5
  712.3 9.2 collective-permute-done.5
  731.6 129.1 %while.35 = (s32[]{:T(128)}, f32[1,512,8,64]{1,3,2,0:T(8,128)}, bf16[8,1,256,512]{3,2,0,1:T(8,128)(2,1)}, bf16[8,1,256,512]{3,2,0,1:T(8,128)(2,1)}, s32[8]{0:T(1...) while((s32[]{:T(128)}, f32[1,512,8,64]{1,3,2,0:T(8,128)}, ...), condition=%wide.wide.region_12.13_spmd.clone, body=%wide.wide.region_11.12_spmd.clone.sunk | while | flops 679871232 | bytes 27977976 | solution.py:278
  862.3 8.3 bitcast_convert_fusion.1
  877.6 13.8 reduce-scatter.17.cloned.1.call-done
  908.3 17.3 %reduce-scatter.19.cloned.1.call-done = bf16[2,1,256,512]{3,2,0,1:T(8,128)(2,1)} async-done(((bf16[8,1,256,512]{3,2,0,1:T(8,128)(2,1)}), bf16[2,1,256,512]{3,2,0,1:T(8,128)(2,1)}) %reduce-scatter.19.cloned.1.call-update) | async-done | bytes 524304 | tf_op jit(solution)/shard_map/reduce_scatter | solution.py:285
  925.6 8.6 fusion.51
  935.9 11.0 fusion.57
  948.6 6.4 bitcast_convert_fusion.2
  956.7 14.6 %bitcast_convert_fusion = bf16[2048,2,2048]{2,0,1:T(8,128)(2,1)} fusion(bf16[2,256,1,2048]{3,1,0,2:T(8,128)(2,1)} %copy-done.39, bf16[2,256,1,2048]{3,1,0,2:T(8,128)(2,1)} %copy-done.38, bf16[1,2,256,2048]{3,2,1,0:T(8,128)(2,1)S(1)} %copy-done.32), kind=kOutput, calls=%fused_computation.58 | convolution fusion | flops 8606711808 | bytes 23068672 | tf_op jit(solution)/shard_map/spcd,spctf->dtf/dot_general | solution.py:213
  973.2 27.2 %reduce-scatter.29.cloned.1.call-done = bf16[2048,256]{1,0:T(8,128)(2,1)} async-done(((bf16[2048,2048]{1,0:T(8,128)(2,1)}), bf16[2048,256]{1,0:T(8,128)(2,1)}) %reduce-scatter.29.cloned.1.call-update) | async-done | bytes 1048592 | tf_op jit(solution)/shard_map/reduce_scatter | solution.py:228
  1003.1 41.6 %reduce-scatter.25.cloned.1.call-done = bf16[512,256]{1,0:T(8,128)(2,1)} async-done(((bf16[512,2048]{1,0:T(8,128)(2,1)}), bf16[512,256]{1,0:T(8,128)(2,1)}) %reduce-scatter.25.cloned.1.call-update) | async-done | bytes 262160 | tf_op jit(solution)/shard_map/reduce_scatter | solution.py:319
  1046.5 77.8 %reduce-scatter.21.cloned.1.call-done = f32[1,2,64,2048]{3,2,1,0:T(8,128)} async-done(((f32[1,2,256,2048]{3,2,1,0:T(8,128)}), f32[1,2,64,2048]{3,2,1,0:T(8,128)}) %reduce-scatter.21.cloned.1.call-update) | async-done | bytes 1048592 | tf_op jit(solution)/shard_map/reduce_scatter | solution.py:68
  1125.8 13.6 all-reduce.3
  1139.6 12.5 all-reduce.2
  1152.1 51.9 %reduce-scatter.13.cloned.1.call-done = f32[1,2,64,2048]{3,2,1,0:T(8,128)} async-done(((f32[1,2,256,2048]{3,2,1,0:T(8,128)}), f32[1,2,64,2048]{3,2,1,0:T(8,128)}) %reduce-scatter.13.cloned.1.call-update) | async-done | bytes 1048592 | tf_op jit(solution)/shard_map/reduce_scatter | solution.py:60
  1204.0 3.1 fusion.79
  1207.1 62.2 %reduce-scatter.23.cloned.1.call-done = bf16[256,3,512]{2,0,1:T(8,128)(2,1)} async-done(((bf16[2048,3,512]{2,0,1:T(8,128)(2,1)}), bf16[256,3,512]{2,0,1:T(8,128)(2,1)}) %reduce-scatter.23.cloned.1.call-update) | async-done | bytes 786448 | tf_op jit(solution)/shard_map/reduce_scatter | solution.py:316
  1271.8 117.2 %reduce-scatter.27.cloned.1.call-done = bf16[256,2,2048]{2,0,1:T(8,128)(2,1)} async-done(((bf16[2048,2,2048]{2,0,1:T(8,128)(2,1)}), bf16[256,2,2048]{2,0,1:T(8,128)(2,1)}) %reduce-scatter.27.cloned.1.call-update) | async-done | bytes 2097168 | tf_op jit(solution)/shard_map/reduce_scatter | solution.py:225
  1389.0 5.8 copy.97
  (434 shorter events, 300.4 us)
Async XLA Ops:
  7.2 15.3 %copy-start.34 = (s32[1,8]{1,0:T(1,128)S(1)}, s32[1,8]{1,0:T(1,128)}, u32[]{:S(2)}) copy-start(s32[1,8]{1,0:T(1,128)} %param.14) | copy-start | bytes 100
  7.2 50.9 %all-gather.13.cloned.1.call-start = ((), (), s32[]{:S(2)}) async-start(), calls=%async_computation.11 | async-start | bytes 7077888 | tf_op jit(solution)/shard_map/all_gather | solution.py:129
  7.9 98.0 %all-gather.11.cloned.1.call-start = ((), (), s32[]{:S(2)}) async-start(), calls=%async_computation.10 | async-start | bytes 2621440 | tf_op jit(solution)/shard_map/all_gather | solution.py:56
  19.0 3.6 copy-start.27
  22.4 121.5 %all-gather.15.cloned.1.call-start = ((), (), s32[]{:S(2)}) async-start(), calls=%async_computation.12 | async-start | bytes 2621440 | tf_op jit(solution)/shard_map/all_gather | solution.py:150
  23.0 103.2 %copy-start.13 = (f32[512,64]{0,1:T(8,128)}, f32[512,64]{0,1:T(8,128)S(1)}, u32[]{:S(2)}) copy-start(f32[512,64]{0,1:T(8,128)S(1)} %get-tuple-element.494) | copy-start | bytes 393220
  23.0 103.2 %copy-start.20 = (f32[512,64]{0,1:T(8,128)}, f32[512,64]{0,1:T(8,128)S(1)}, u32[]{:S(2)}) copy-start(f32[512,64]{0,1:T(8,128)S(1)} %get-tuple-element.493) | copy-start | bytes 393220
  24.9 41.9 %copy-start.7 = (f32[512,8,64]{0,2,1:T(8,128)}, f32[512,8,64]{0,2,1:T(8,128)S(1)}, u32[]{:S(2)}) copy-start(f32[512,8,64]{0,2,1:T(8,128)S(1)} %mul.381) | copy-start | bytes 3145732
  122.3 3.9 copy-start.24
  122.3 46.1 %all-gather.17.cloned.1.call-start = ((), (), s32[]{:S(2)}) async-start(), calls=%async_computation.13 | async-start | bytes 2621440 | tf_op jit(solution)/shard_map/all_gather | solution.py:151
  125.3 140.1 %all-gather.19.cloned.1.call-start = ((), (), s32[]{:S(2)}) async-start(), calls=%async_computation.14 | async-start | bytes 2359296 | tf_op jit(solution)/shard_map/all_gather | solution.py:130
  125.9 221.8 %reduce-scatter.11.cloned.1.call-start = ((), (), s32[]{:S(2)}) async-start(), calls=%async_computation.15 | async-start | bytes 5242880 | tf_op jit(solution)/shard_map/reduce_scatter | solution.py:60
  177.9 3.5 copy-start
  189.5 3.5 copy-start
  201.0 3.5 copy-start
  212.6 3.5 copy-start
  224.2 3.5 copy-start
  265.4 5.1 copy-start.22
  270.5 77.2 %copy-start.3 = (bf16[1,2,64,2048]{3,2,1,0:T(8,128)(2,1)S(1)}, bf16[1,2,64,2048]{3,2,1,0:T(8,128)(2,1)}, u32[]{:S(2)}) copy-start(bf16[1,2,64,2048]{3,2,1,0:T(8,128)(2,1)} %param.13) | copy-start | bytes 1572868
  270.5 156.4 %all-gather.21.cloned.1.call-start = ((), (), s32[]{:S(2)}) async-start(), calls=%async_computation.16 | async-start | bytes 2621440 | tf_op jit(solution)/shard_map/all_gather | solution.py:56
  349.2 331.9 %copy-start.1 = (f32[1,2,64,2048]{3,2,1,0:T(8,128)}, f32[1,2,64,2048]{3,2,1,0:T(8,128)S(1)}, u32[]{:S(2)}) copy-start(f32[1,2,64,2048]{3,2,1,0:T(8,128)S(1)} %get-tuple-element.462) | copy-start | bytes 3145732
  350.3 167.0 %all-gather.23.cloned.1.call-start = ((), (), s32[]{:S(2)}) async-start(), calls=%async_computation.17 | async-start | bytes 18874368 | tf_op jit(solution)/shard_map/all_gather | solution.py:186
  354.2 221.0 %all-gather.25.cloned.1.call-start = ((), (), s32[]{:S(2)}) async-start(), calls=%async_computation.18 | async-start | bytes 9437184 | tf_op jit(solution)/shard_map/all_gather | solution.py:187
  354.9 324.2 %reduce-scatter.15.cloned.1.call-start = ((), (), s32[]{:S(2)}) async-start(), calls=%async_computation.20 | async-start | bytes 5242880 | tf_op jit(solution)/shard_map/reduce_scatter | solution.py:68
  355.2 25.4 %collective-permute-start = (bf16[1,2,64,2048]{3,2,1,0:T(8,128)(2,1)S(1)}, bf16[1,2,64,2048]{3,2,1,0:T(8,128)(2,1)}, u32[]{:S(2)}, u32[]{:S(2)}) collective-permute-start(bf16[1,2,64,2048]{3,2,1,0:T(8,128)(2,1)S(1)} %copy-done.9), channel_id=1, source_target_pairs={{0,1},{1,2},{2,3},{3,0},{4,5},{5,6},{6,7},{7,4},{8,9},{9,10},{10,1... | collective-permute-start | bytes 1572872 | tf_op jit(solution)/shard_map/ppermute | solution.py:18
  356.7 50.6 %collective-permute-start.1 = (bf16[1,2,64,2048]{3,2,1,0:T(8,128)(2,1)S(1)}, bf16[1,2,64,2048]{3,2,1,0:T(8,128)(2,1)}, u32[]{:S(2)}, u32[]{:S(2)}) collective-permute-start(bf16[1,2,64,2048]{3,2,1,0:T(8,128)(2,1)S(1)} %copy-done.9), channel_id=1, source_target_pairs={{0,3},{1,0},{2,1},{3,2},{4,7},{5,4},{6,5},{7,6},{8,11},{9,8},{10,9... | collective-permute-start | bytes 1572872 | tf_op jit(solution)/shard_map/ppermute | solution.py:21
  380.6 43.4 %collective-permute-start.2 = (bf16[1,2,64,2048]{3,2,1,0:T(8,128)(2,1)}, bf16[1,2,64,2048]{3,2,1,0:T(8,128)(2,1)S(1)}, u32[]{:S(2)}, u32[]{:S(2)}) collective-permute-start(bf16[1,2,64,2048]{3,2,1,0:T(8,128)(2,1)} %collective-permute-done), channel_id=1, source_target_pairs={{0,1},{1,2},{2,3},{3,0},{4,5},{5,6},{6,7},{7,4},{8,9},{9,10},{10,1... | collective-permute-start | bytes 1572872 | tf_op jit(solution)/shard_map/ppermute | solution.py:18
  602.2 289.2 %reduce-scatter.17.cloned.1.call-start = ((), (), s32[]{:S(2)}) async-start(), calls=%async_computation.21 | async-start | bytes 2621440 | tf_op jit(solution)/shard_map/reduce_scatter | solution.py:282
  683.6 16.9 %collective-permute-start.3 = (bf16[1,2,64,2048]{3,2,1,0:T(8,128)(2,1)}, bf16[1,2,64,2048]{3,2,1,0:T(8,128)(2,1)S(1)}, u32[]{:S(2)}, u32[]{:S(2)}) collective-permute-start(bf16[1,2,64,2048]{3,2,1,0:T(8,128)(2,1)} %get-tuple-element.460), channel_id=1, source_target_pairs={{0,1},{1,2},{2,3},{3,0},{4,5},{5,6},{6,7},{7,4},{8,9},{9,10},{10,1... | collective-permute-start | bytes 1572872 | tf_op jit(solution)/shard_map/ppermute | solution.py:18
  685.1 37.2 %copy-start.17 = (bf16[512,2048]{1,0:T(8,128)(2,1)S(1)}, bf16[512,2048]{1,0:T(8,128)(2,1)}, u32[]{:S(2)}) copy-start(bf16[512,2048]{1,0:T(8,128)(2,1)} %all-gather.19.cloned.1.call-done) | copy-start | bytes 6291460
  685.1 26.4 %collective-permute-start.4 = (bf16[1,2,64,2048]{3,2,1,0:T(8,128)(2,1)}, bf16[1,2,64,2048]{3,2,1,0:T(8,128)(2,1)S(1)}, u32[]{:S(2)}, u32[]{:S(2)}) collective-permute-start(bf16[1,2,64,2048]{3,2,1,0:T(8,128)(2,1)} %get-tuple-element.460), channel_id=1, source_target_pairs={{0,3},{1,0},{2,1},{3,2},{4,7},{5,4},{6,5},{7,6},{8,11},{9,8},{10,9... | collective-permute-start | bytes 1572872 | tf_op jit(solution)/shard_map/ppermute | solution.py:21
  700.5 21.0 %collective-permute-start.5 = (bf16[1,2,64,2048]{3,2,1,0:T(8,128)(2,1)S(1)}, bf16[1,2,64,2048]{3,2,1,0:T(8,128)(2,1)S(1)}, u32[]{:S(2)}, u32[]{:S(2)}) collective-permute-start(bf16[1,2,64,2048]{3,2,1,0:T(8,128)(2,1)S(1)} %collective-permute-done.3), channel_id=1, source_target_pairs={{0,1},{1,2},{2,3},{3,0},{4,5},{5,6},{6,7},{7,4},{8,9},{9,10},{10,1... | collective-permute-start | bytes 1572872 | tf_op jit(solution)/shard_map/ppermute | solution.py:18
  860.7 64.9 %reduce-scatter.19.cloned.1.call-start = ((), (), s32[]{:S(2)}) async-start(), calls=%async_computation.22 | async-start | bytes 2621440 | tf_op jit(solution)/shard_map/reduce_scatter | solution.py:285
  861.3 139.1 %reduce-scatter.29.cloned.1.call-start = ((), (), s32[]{:S(2)}) async-start(), calls=%async_computation.27 | async-start | bytes 9437184 | tf_op jit(solution)/shard_map/reduce_scatter | solution.py:228
  870.6 174.0 %reduce-scatter.25.cloned.1.call-start = ((), (), s32[]{:S(2)}) async-start(), calls=%async_computation.25 | async-start | bytes 2359296 | tf_op jit(solution)/shard_map/reduce_scatter | solution.py:319
  874.9 249.3 %reduce-scatter.21.cloned.1.call-start = ((), (), s32[]{:S(2)}) async-start(), calls=%async_computation.23 | async-start | bytes 5242880 | tf_op jit(solution)/shard_map/reduce_scatter | solution.py:68
  877.6 16.9 %copy-start.14 = (f32[512,64]{0,1:T(8,128)S(1)}, f32[512,64]{0,1:T(8,128)}, u32[]{:S(2)}) copy-start(f32[512,64]{0,1:T(8,128)} %copy-done.13) | copy-start | bytes 393220
  902.2 5.0 copy-start.19
  907.2 18.4 %copy-start.25 = (bf16[2,256,1,512]{3,1,2,0:T(8,128)(2,1)S(1)}, bf16[2,256,1,512]{3,1,2,0:T(8,128)(2,1)}, u32[]{:S(2)}) copy-start(bf16[2,256,1,512]{3,1,2,0:T(8,128)(2,1)} %copy.91) | copy-start | bytes 1572868
  934.2 269.8 %reduce-scatter.13.cloned.1.call-start = ((), (), s32[]{:S(2)}) async-start(), calls=%async_computation.19 | async-start | bytes 5242880 | tf_op jit(solution)/shard_map/reduce_scatter | solution.py:60
  946.9 322.4 %reduce-scatter.23.cloned.1.call-start = ((), (), s32[]{:S(2)}) async-start(), calls=%async_computation.24 | async-start | bytes 7077888 | tf_op jit(solution)/shard_map/reduce_scatter | solution.py:316
  955.1 433.9 %reduce-scatter.27.cloned.1.call-start = ((), (), s32[]{:S(2)}) async-start(), calls=%async_computation.26 | async-start | bytes 18874368 | tf_op jit(solution)/shard_map/reduce_scatter | solution.py:225
  971.3 152.9 %copy-start.4 = (bf16[1,2,64,2048]{3,2,1,0:T(8,128)(2,1)S(1)}, bf16[1,2,64,2048]{3,2,1,0:T(8,128)(2,1)}, u32[]{:S(2)}) copy-start(bf16[1,2,64,2048]{3,2,1,0:T(8,128)(2,1)} %param.13) | copy-start | bytes 1572868
  971.3 152.9 %copy-start.28 = (f32[8,1,256]{2,1,0:T(1,128)S(1)}, f32[8,1,256]{2,1,0:T(1,128)}, u32[]{:S(2)}) copy-start(f32[8,1,256]{2,1,0:T(1,128)} %copy-done.27) | copy-start | bytes 24580
  971.3 152.9 %copy-start.30 = (f32[2,64]{1,0:T(2,128)S(1)}, f32[2,64]{1,0:T(2,128)}, u32[]{:S(2)}) copy-start(f32[2,64]{1,0:T(2,128)} %copy-done.29) | copy-start | bytes 1540
  973.1 230.8 %copy-start.2 = (f32[1,2,64,2048]{3,2,1,0:T(8,128)S(1)}, f32[1,2,64,2048]{3,2,1,0:T(8,128)}, u32[]{:S(2)}) copy-start(f32[1,2,64,2048]{3,2,1,0:T(8,128)} %copy-done.1) | copy-start | bytes 3145732
  973.2 230.8 %copy-start.6 = (f32[1,2,64,2048]{3,2,1,0:T(8,128)S(1)}, f32[1,2,64,2048]{3,2,1,0:T(8,128)}, u32[]{:S(2)}) copy-start(f32[1,2,64,2048]{3,2,1,0:T(8,128)} %reduce-scatter.15.cloned.1.call-done) | copy-start | bytes 3145732
  973.2 230.8 %copy-start.10 = (bf16[1,2,64,2048]{3,2,1,0:T(8,128)(2,1)S(1)}, bf16[1,2,64,2048]{3,2,1,0:T(8,128)(2,1)}, u32[]{:S(2)}) copy-start(bf16[1,2,64,2048]{3,2,1,0:T(8,128)(2,1)} %param.21) | copy-start | bytes 1572868
  (23 other events, 42.6 us)
Sparse Core Ops, SparseCore 0:
  9.9 48.1 all-gather.12
  60.2 45.6 all-gather.10
  122.5 21.3 all-gather.14
  145.9 22.5 all-gather.16
  170.2 28.0 all-gather.18
  270.6 77.0 reduce-scatter.10
  350.5 76.4 all-gather.20
  429.4 87.9 all-gather.22
  519.3 55.8 all-gather.24
  602.3 76.7 reduce-scatter.14
  860.8 30.5 reduce-scatter.16
  894.4 31.1 reduce-scatter.18
  929.0 71.2 reduce-scatter.28
  1003.5 41.1 reduce-scatter.24
  1047.4 76.7 reduce-scatter.20
  1126.4 77.5 reduce-scatter.12
  1207.2 62.0 reduce-scatter.22
  1272.7 116.1 reduce-scatter.26
